TPU v7x, 32 devices: a whole 2x2x4 slice. The times are simulated.
32 devices in a mesh: section: 4 (over x, core), tp: 8 (over z, y).
Axes of the slice: x: 2, y: 2, z: 4, core: 2. Of those that a mesh axis runs over, the one named last changes fastest.
Arguments:
- pending_activation: bfloat16 [4, 128, 4096], P('section'), may hold values from -6 to 6
- admissible_microbatches: bfloat16 [4, 128, 4096], P(None, None, 'tp'), may hold values from -6 to 6
- arrival_plan: int32 [4], replicated, may hold values from 0 to 3, each once
- vanished_hop: int32 [1], replicated, may hold values from 1 to 3
- query_key_value_matrices: bfloat16 [4, 4096, 3, 2048], P('section', None, None, 'tp')
- mixing_projection_matrices: bfloat16 [4, 2048, 4096], P('section', 'tp'), may hold values from -0.125 to 0.125
- normalizer_factors: bfloat16 [4, 4096], P('section'), may hold values from 0.25 to 1.75
Outputs:
- activation_later: bfloat16 [4, 128, 4096], P('section')
- standby_input: bfloat16 [4, 128, 4096], P('section', None, 'tp')
Inputs may be any that keep to these rules, and one draw needn't show every extreme that they name: `vanished_hop`: the preempted section is not the first. `arrival_plan`: each micro-batch index once.
All inputs are finite; a program needn't handle non-finite values.
Results may differ from a plain program's by a relative error of at most 0.013.
Values may be sent and summed in bfloat16 or wider, within the bound.
A program may use at most 64 MiB of HBM per device.

v0:
```python
import jax
import jax.numpy as jnp
from jax import lax
from jax.sharding import PartitionSpec as P

HD = 128
TICKS = 3
NORM_EPS = 1e-05


def shifted(value, axis, steps):
    count = lax.axis_size(axis)
    pairs = [(source, (source + steps) % count) for source in range(count)]
    return lax.ppermute(value, axis, pairs)


def layer_norm(x_rows, scale_row):
    widened = x_rows.astype(jnp.float32)
    row_mean = jnp.mean(widened, axis=-1, keepdims=True)
    centered = widened - row_mean
    row_var = jnp.mean(centered * centered, axis=-1, keepdims=True)
    return (centered * lax.rsqrt(row_var + NORM_EPS) * scale_row.astype(jnp.float32)).astype(
        jnp.bfloat16
    )


def attend(normed, w_in, w_out):
    row_count = normed.shape[0]
    col_count = w_in.shape[2]
    head_count = col_count // HD
    projected = jnp.dot(
        normed, w_in.reshape(w_in.shape[0], 3 * col_count), preferred_element_type=jnp.float32
    )
    projected = projected.astype(jnp.bfloat16).reshape(row_count, 3, head_count, HD)
    queries = projected[:, 0]
    key_rows = projected[:, 1]
    values = projected[:, 2]
    scores = jnp.einsum(
        "qhd,khd->hqk", queries, key_rows, preferred_element_type=jnp.float32
    ) * HD ** (-0.5)
    causal = jnp.arange(row_count)[:, None] >= jnp.arange(row_count)[None, :]
    scores = jnp.where(causal[None], scores, -jnp.inf)
    row_max = jnp.max(scores, axis=-1, keepdims=True)
    weights = jnp.exp(scores - row_max)
    probs = (weights / jnp.sum(weights, axis=-1, keepdims=True)).astype(jnp.bfloat16)
    context = jnp.einsum("hqk,khd->qhd", probs, values, preferred_element_type=jnp.float32)
    context = context.astype(jnp.bfloat16).reshape(row_count, col_count)
    return jnp.dot(context, w_out, preferred_element_type=jnp.float32)


def per_device(
    pending_activation,
    admissible_microbatches,
    arrival_plan,
    vanished_hop,
    query_key_value_matrices,
    mixing_projection_matrices,
    normalizer_factors,
):
    sections = lax.axis_size("section")
    my_section = lax.axis_index("section")
    sharding_degree = lax.axis_size("tp")
    slice_breadth = pending_activation.shape[2] // sharding_degree
    col_start = lax.axis_index("tp") * slice_breadth
    lost_at = vanished_hop[0]
    is_pred = my_section == lost_at - 1
    is_next = my_section == lost_at + 1
    is_lost = my_section == lost_at
    w_in = query_key_value_matrices[0]
    w_out = mixing_projection_matrices[0]
    scale_row = normalizer_factors[0]
    entire_source_lines = pending_activation[0]
    x_sh = lax.dynamic_slice_in_dim(entire_source_lines, col_start, slice_breadth, 1)
    blank = jnp.zeros(entire_source_lines.shape, jnp.float32)
    far_in, far_out, far_gain = shifted((w_in, w_out, scale_row), "section", -1)

    def successor_layer(rows_full):
        return attend(layer_norm(rows_full, far_gain), far_in, far_out)

    standby_sh = x_sh
    for tick_index in range(TICKS):
        own_part = attend(layer_norm(entire_source_lines, scale_row), w_in, w_out)
        ya_sh = (
            x_sh.astype(jnp.float32)
            + lax.psum_scatter(own_part, "tp", scatter_dimension=1, tiled=True)
        ).astype(jnp.bfloat16)
        ya_full = lax.all_gather(ya_sh, "tp", axis=1, tiled=True)
        spare_part = (
            successor_layer(ya_full)
            if tick_index == TICKS - 1
            else lax.cond(is_pred, lambda: successor_layer(ya_full), lambda: blank)
        )
        spare_sh = (
            ya_sh.astype(jnp.float32)
            + lax.psum_scatter(spare_part, "tp", scatter_dimension=1, tiled=True)
        ).astype(jnp.bfloat16)
        result_sh = jnp.where(is_pred, spare_sh, ya_sh)
        entering = lax.dynamic_index_in_dim(
            admissible_microbatches, arrival_plan[tick_index], 0, keepdims=False
        )
        send_sh = jnp.where(my_section == sections - 1, entering, result_sh)
        near_rows = shifted(send_sh, "section", 1)
        far_rows = shifted(spare_sh, "section", 2)
        x_sh = jnp.where(is_lost, jnp.zeros_like(far_rows), jnp.where(is_next, far_rows, near_rows))
        entire_source_lines = lax.all_gather(x_sh, "tp", axis=1, tiled=True)
        standby_sh = far_rows
    return (entire_source_lines[None], standby_sh[None])


def solution(mesh):
    placed = (
        P("section", None, None),
        P(None, None, "tp"),
        P(),
        P(),
        P("section", None, None, "tp"),
        P("section", "tp", None),
        P("section", None),
    )
    return jax.shard_map(
        per_device,
        mesh=mesh,
        in_specs=placed,
        out_specs=(P("section", None, None), P("section", None, "tp")),
        check_vma=False,
    )
```

profile of v0, /device:TPU:0, one launch (start us, length us, event | category | flops | bytes accessed | tf_op | source)
XLA Modules:
  0.0 769.3 jit_solution(308551706380850222)
XLA Ops:
  7.2 8.8 %copy.42 = bf16[1,4096,3,256]{1,3,2,0:T(8,128)(2,1)} copy(bf16[1,4096,3,256]{3,1,2,0:T(8,128)(2,1)} %param.15) | data formatting | bytes 12582912 | tf_op args[4]
  16.1 2.4 collective-permute-start.1
  18.5 0.6 iota_compare_fusion.2
  19.9 5.2 convolution_convert_fusion.7
  25.2 0.9 fusion.65
  26.5 1.8 fusion.103
  28.4 0.7 collective-permute-start.2
  29.1 68.7 %reduce-scatter.7.cloned.1.call-done = f32[128,512]{1,0:T(8,128)} async-done(((f32[128,4096]{1,0:T(8,128)}), f32[128,512]{1,0:T(8,128)}) %reduce-scatter.7.cloned.1.call-update) | async-done | bytes 262160 | tf_op jit(solution)/shard_map/reduce_scatter | solution.py:85
  97.8 1.6 fusion.86
  100.3 9.4 %collective-permute-done = bf16[4096]{0:T(1024)(128)(2,1)S(1)} collective-permute-done((bf16[4096]{0:T(1024)(128)(2,1)S(1)}, bf16[4096]{0:T(1024)(128)(2,1)S(1)}, u32[]{:S(2)}, u32[]{:S(2)}) %collective-permute-start) | collective-permute-done | bytes 8224 | tf_op jit(solution)/shard_map/ppermute | solution.py:14
  109.7 29.2 %all-gather.7.cloned.1.call-done = bf16[128,4096]{1,0:T(8,128)(2,1)} async-done(((bf16[128,512]{1,0:T(8,128)(2,1)}), bf16[128,4096]{1,0:T(8,128)(2,1)}) %all-gather.7.cloned.1.call-update) | async-done | bytes 1048592 | tf_op jit(solution)/shard_map/all_gather | solution.py:87
  138.9 12.4 %conditional.2 = (f32[128,4096]{1,0:T(8,128)}) conditional(s32[]{:T(128)} %convert_element_type.183, () %tuple.20, (bf16[128,4096]{1,0:T(8,128)(2,1)}, bf16[4096]{0:T(1024)(128)(2,1)S(1)}, bf16[4096,3,256]{0,2,1:T(8,128)(2,1)}, bf16[256,4096]{1,0:T(8,128)(2,1)}) %tuple.21), branch_computations={%region_5.6_spmd, %region_6.11_spmd} | conditional | flops 1096667776 | bytes 19741220 | solution.py:91
  138.9 1.5 convert_reduce_fusion
  140.5 1.7 fusion.3
  142.2 5.0 convolution_convert_fusion
  148.0 3.4 fusion.118
  151.5 0.6 copy-done.17
  152.0 0.7 fusion.113
  154.6 64.0 %reduce-scatter.9.cloned.1.call-done = f32[128,512]{1,0:T(8,128)} async-done(((f32[128,4096]{1,0:T(8,128)}), f32[128,512]{1,0:T(8,128)}) %reduce-scatter.9.cloned.1.call-update) | async-done | bytes 262160 | tf_op jit(solution)/shard_map/reduce_scatter | solution.py:95
  218.5 1.1 bitcast_select_fusion.2
  219.6 1.5 collective-permute-start.3
  221.2 4.0 collective-permute-done.3
  225.2 0.9 collective-permute-done.4
  226.1 0.7 select_select_fusion.2
  226.8 38.5 %all-gather.9.cloned.1.call-done = bf16[128,4096]{1,0:T(8,128)(2,1)} async-done(((bf16[128,512]{1,0:T(8,128)(2,1)}), bf16[128,4096]{1,0:T(8,128)(2,1)}) %all-gather.9.cloned.1.call-update) | async-done | bytes 1048592 | tf_op jit(solution)/shard_map/all_gather | solution.py:105
  265.3 1.5 convert_reduce_fusion.5
  266.9 1.7 fusion.48
  268.6 5.0 convolution_convert_fusion.6
  274.4 1.8 fusion.101
  276.2 68.0 %reduce-scatter.11.cloned.1.call-done = f32[128,512]{1,0:T(8,128)} async-done(((f32[128,4096]{1,0:T(8,128)}), f32[128,512]{1,0:T(8,128)}) %reduce-scatter.11.cloned.1.call-update) | async-done | bytes 262160 | tf_op jit(solution)/shard_map/reduce_scatter | solution.py:85
  344.2 1.6 add_convert_fusion.3
  346.0 39.2 %all-gather.11.cloned.1.call-done = bf16[128,4096]{1,0:T(8,128)(2,1)} async-done(((bf16[128,512]{1,0:T(8,128)(2,1)}), bf16[128,4096]{1,0:T(8,128)(2,1)}) %all-gather.11.cloned.1.call-update) | async-done | bytes 1048592 | tf_op jit(solution)/shard_map/all_gather | solution.py:87
  385.2 12.4 %conditional.3 = (f32[128,4096]{1,0:T(8,128)}) conditional(s32[]{:T(128)} %convert_element_type.183, () %tuple.22, (bf16[128,4096]{1,0:T(8,128)(2,1)}, bf16[4096]{0:T(1024)(128)(2,1)S(1)}, bf16[4096,3,256]{0,2,1:T(8,128)(2,1)}, bf16[256,4096]{1,0:T(8,128)(2,1)}) %tuple.23), branch_computations={%region_17.18_spmd, %region_18.23_spmd} | conditional | flops 1096667776 | bytes 19741220 | solution.py:91
  385.2 1.5 convert_reduce_fusion.1
  386.7 1.7 fusion.19
  388.4 5.0 convolution_convert_fusion.2
  394.2 3.4 fusion.119
  399.6 65.4 %reduce-scatter.13.cloned.1.call-done = f32[128,512]{1,0:T(8,128)} async-done(((f32[128,4096]{1,0:T(8,128)}), f32[128,512]{1,0:T(8,128)}) %reduce-scatter.13.cloned.1.call-update) | async-done | bytes 262160 | tf_op jit(solution)/shard_map/reduce_scatter | solution.py:95
  465.1 1.0 bitcast_select_fusion.1
  466.1 1.5 collective-permute-start.5
  467.6 4.0 collective-permute-done.5
  471.6 0.9 collective-permute-done.6
  472.5 0.7 select_select_fusion.1
  473.3 38.5 %all-gather.13.cloned.1.call-done = bf16[128,4096]{1,0:T(8,128)(2,1)} async-done(((bf16[128,512]{1,0:T(8,128)(2,1)}), bf16[128,4096]{1,0:T(8,128)(2,1)}) %all-gather.13.cloned.1.call-update) | async-done | bytes 1048592 | tf_op jit(solution)/shard_map/all_gather | solution.py:105
  511.8 1.5 convert_reduce_fusion.4
  513.3 1.7 fusion.45
  515.0 5.0 convolution_convert_fusion.5
  520.8 1.8 fusion.99
  522.7 68.3 %reduce-scatter.15.cloned.1.call-done = f32[128,512]{1,0:T(8,128)} async-done(((f32[128,4096]{1,0:T(8,128)}), f32[128,512]{1,0:T(8,128)}) %reduce-scatter.15.cloned.1.call-update) | async-done | bytes 262160 | tf_op jit(solution)/shard_map/reduce_scatter | solution.py:85
  591.0 1.6 add_convert_fusion.1
  592.7 39.2 %all-gather.15.cloned.1.call-done = bf16[128,4096]{1,0:T(8,128)(2,1)} async-done(((bf16[128,512]{1,0:T(8,128)(2,1)}), bf16[128,4096]{1,0:T(8,128)(2,1)}) %all-gather.15.cloned.1.call-update) | async-done | bytes 1048592 | tf_op jit(solution)/shard_map/all_gather | solution.py:87
  631.9 1.5 convert_reduce_fusion.3
  633.5 1.7 fusion.42
  635.2 5.0 convolution_convert_fusion.4
  640.9 3.4 fusion.120
  646.5 66.3 %reduce-scatter.17.cloned.1.call-done = f32[128,512]{1,0:T(8,128)} async-done(((f32[128,4096]{1,0:T(8,128)}), f32[128,512]{1,0:T(8,128)}) %reduce-scatter.17.cloned.1.call-update) | async-done | bytes 262160 | tf_op jit(solution)/shard_map/reduce_scatter | solution.py:95
  712.8 1.0 bitcast_select_fusion
  713.8 1.5 collective-permute-start.7
  715.3 4.1 collective-permute-done.7
  719.4 0.9 collective-permute-done.8
  720.2 0.7 select_select_fusion
  720.9 38.5 %all-gather.17.cloned.1.call-done = bf16[128,4096]{1,0:T(8,128)(2,1)} async-done(((bf16[128,512]{1,0:T(8,128)(2,1)}), bf16[128,4096]{1,0:T(8,128)(2,1)}) %all-gather.17.cloned.1.call-update) | async-done | bytes 1048592 | tf_op jit(solution)/shard_map/all_gather | solution.py:105
  759.5 2.3 copy.115
  761.8 0.7 copy.116
  (121 shorter events, 5.9 us)
Async XLA Ops:
  7.2 11.9 %copy-start.15 = (bf16[1,4096]{1,0:T(2,128)(2,1)S(1)}, bf16[1,4096]{1,0:T(2,128)(2,1)}, u32[]{:S(2)}) copy-start(bf16[1,4096]{1,0:T(2,128)(2,1)} %param.17) | copy-start | bytes 24580
  7.2 12.0 %copy-start.1 = (bf16[1,128,4096]{2,1,0:T(8,128)(2,1)S(1)}, bf16[1,128,4096]{2,1,0:T(8,128)(2,1)}, u32[]{:S(2)}) copy-start(bf16[1,128,4096]{2,1,0:T(8,128)(2,1)} %param.11) | copy-start | bytes 3145732
  7.2 90.7 %reduce-scatter.7.cloned.1.call-start = ((), (), s32[]{:S(2)}) async-start(), calls=%async_computation.6 | async-start | bytes 2359296 | tf_op jit(solution)/shard_map/reduce_scatter | solution.py:85
  16.1 122.9 %collective-permute-start.1 = (bf16[4096,3,256]{0,2,1:T(8,128)(2,1)}, bf16[4096,3,256]{0,2,1:T(8,128)(2,1)}, u32[]{:S(2)}, u32[]{:S(2)}) collective-permute-start(bf16[4096,3,256]{0,2,1:T(8,128)(2,1)} %bitcast.141), channel_id=1, source_target_pairs={{0,24},{8,0},{16,8},{24,16},{1,25},{9,1},{17,9},{25,17},{2,26},{10... | collective-permute-start | bytes 18874376 | tf_op jit(solution)/shard_map/ppermute | solution.py:14
  19.2 0.7 copy-start.13
  19.8 6.7 copy-start
  28.3 110.6 %all-gather.7.cloned.1.call-start = ((), (), s32[]{:S(2)}) async-start(), calls=%async_computation.7 | async-start | bytes 1179648 | tf_op jit(solution)/shard_map/all_gather | solution.py:87
  28.4 81.3 %collective-permute-start.2 = (bf16[256,4096]{1,0:T(8,128)(2,1)S(1)}, bf16[256,4096]{1,0:T(8,128)(2,1)}, u32[]{:S(2)}, u32[]{:S(2)}) collective-permute-start(bf16[256,4096]{1,0:T(8,128)(2,1)S(1)} %bitcast.140), channel_id=1, source_target_pairs={{0,24},{8,0},{16,8},{24,16},{1,25},{9,1},{17,9},{25,17},{2,26},{10... | collective-permute-start | bytes 6291464 | tf_op jit(solution)/shard_map/ppermute | solution.py:14
  99.5 119.0 %reduce-scatter.9.cloned.1.call-start = ((), (), s32[]{:S(2)}) async-start(), calls=%async_computation.8 | async-start | bytes 2359296 | tf_op jit(solution)/shard_map/reduce_scatter | solution.py:95
  99.6 10.2 %collective-permute-start = (bf16[4096]{0:T(1024)(128)(2,1)S(1)}, bf16[4096]{0:T(1024)(128)(2,1)S(1)}, u32[]{:S(2)}, u32[]{:S(2)}) collective-permute-start(bf16[4096]{0:T(1024)(128)(2,1)S(1)} %reduce.1), channel_id=1, source_target_pairs={{0,24},{8,0},{16,8},{24,16},{1,25},{9,1},{17,9},{25,17},{2,26},{10... | collective-permute-start | bytes 24584 | tf_op jit(solution)/shard_map/ppermute | solution.py:14
  138.9 3.2 copy-start.2
  151.4 0.7 copy-start.17
  151.4 67.2 %copy-start.7 = (bf16[128,512]{1,0:T(8,128)(2,1)S(1)}, bf16[128,512]{1,0:T(8,128)(2,1)}, u32[]{:S(2)}) copy-start(bf16[128,512]{1,0:T(8,128)(2,1)} %fusion.86) | copy-start | bytes 393220
  151.4 117.1 %copy-start.14 = (f32[4096]{0:T(1024)S(1)}, f32[4096]{0:T(1024)}, u32[]{:S(2)}) copy-start(f32[4096]{0:T(1024)} %copy-done.13) | copy-start | bytes 49156
  151.4 113.9 %all-gather.9.cloned.1.call-start = ((), (), s32[]{:S(2)}) async-start(), calls=%async_computation.9 | async-start | bytes 1179648 | tf_op jit(solution)/shard_map/all_gather | solution.py:105
  219.6 5.5 collective-permute-start.3
  221.2 4.9 collective-permute-start.4
  226.8 117.5 %reduce-scatter.11.cloned.1.call-start = ((), (), s32[]{:S(2)}) async-start(), calls=%async_computation.10 | async-start | bytes 2359296 | tf_op jit(solution)/shard_map/reduce_scatter | solution.py:85
  265.3 3.2 copy-start.6
  268.6 5.3 copy-start.16
  276.2 68.1 %copy-start.9 = (bf16[128,512]{1,0:T(8,128)(2,1)S(1)}, bf16[128,512]{1,0:T(8,128)(2,1)}, u32[]{:S(2)}) copy-start(bf16[128,512]{1,0:T(8,128)(2,1)} %select_select_fusion.2) | copy-start | bytes 393220
  276.2 109.0 %all-gather.11.cloned.1.call-start = ((), (), s32[]{:S(2)}) async-start(), calls=%async_computation.11 | async-start | bytes 1179648 | tf_op jit(solution)/shard_map/all_gather | solution.py:87
  345.9 119.2 %reduce-scatter.13.cloned.1.call-start = ((), (), s32[]{:S(2)}) async-start(), calls=%async_computation.12 | async-start | bytes 2359296 | tf_op jit(solution)/shard_map/reduce_scatter | solution.py:95
  385.2 3.2 copy-start.3
  397.6 67.5 %copy-start.10 = (bf16[128,512]{1,0:T(8,128)(2,1)S(1)}, bf16[128,512]{1,0:T(8,128)(2,1)}, u32[]{:S(2)}) copy-start(bf16[128,512]{1,0:T(8,128)(2,1)} %add_convert_fusion.3) | copy-start | bytes 393220
  397.6 67.5 %copy-start.12 = (bf16[4,128,512]{2,1,0:T(8,128)(2,1)S(1)}, bf16[4,128,512]{2,1,0:T(8,128)(2,1)}, u32[]{:S(2)}) copy-start(bf16[4,128,512]{2,1,0:T(8,128)(2,1)} %param.12) | copy-start | bytes 1572868
  397.6 114.2 %all-gather.13.cloned.1.call-start = ((), (), s32[]{:S(2)}) async-start(), calls=%async_computation.13 | async-start | bytes 1179648 | tf_op jit(solution)/shard_map/all_gather | solution.py:105
  466.1 5.5 collective-permute-start.5
  467.6 4.9 collective-permute-start.6
  473.2 117.7 %reduce-scatter.15.cloned.1.call-start = ((), (), s32[]{:S(2)}) async-start(), calls=%async_computation.14 | async-start | bytes 2359296 | tf_op jit(solution)/shard_map/reduce_scatter | solution.py:85
  511.8 3.2 copy-start.5
  522.6 68.4 %copy-start.8 = (bf16[128,512]{1,0:T(8,128)(2,1)S(1)}, bf16[128,512]{1,0:T(8,128)(2,1)}, u32[]{:S(2)}) copy-start(bf16[128,512]{1,0:T(8,128)(2,1)} %select_select_fusion.1) | copy-start | bytes 393220
  522.6 109.3 %all-gather.15.cloned.1.call-start = ((), (), s32[]{:S(2)}) async-start(), calls=%async_computation.15 | async-start | bytes 1179648 | tf_op jit(solution)/shard_map/all_gather | solution.py:87
  592.6 120.1 %reduce-scatter.17.cloned.1.call-start = ((), (), s32[]{:S(2)}) async-start(), calls=%async_computation.16 | async-start | bytes 2359296 | tf_op jit(solution)/shard_map/reduce_scatter | solution.py:95
  631.9 3.2 copy-start.4
  644.4 68.4 %copy-start.11 = (bf16[128,512]{1,0:T(8,128)(2,1)S(1)}, bf16[128,512]{1,0:T(8,128)(2,1)}, u32[]{:S(2)}) copy-start(bf16[128,512]{1,0:T(8,128)(2,1)} %add_convert_fusion.1) | copy-start | bytes 393220
  644.4 115.1 %all-gather.17.cloned.1.call-start = ((), (), s32[]{:S(2)}) async-start(), calls=%async_computation.17 | async-start | bytes 1179648 | tf_op jit(solution)/shard_map/all_gather | solution.py:105
  713.8 5.6 collective-permute-start.7
  715.3 4.9 collective-permute-start.8
Sparse Core Ops, SparseCore 0:
  28.5 69.3 reduce-scatter.6
  100.5 38.4 all-gather.6
  151.5 66.9 reduce-scatter.8
  226.9 38.3 all-gather.8
  276.3 67.8 reduce-scatter.10
  346.7 38.3 all-gather.10
  397.7 67.2 reduce-scatter.12
  473.4 38.3 all-gather.12
  522.8 68.1 reduce-scatter.14
  593.4 38.4 all-gather.14
  644.5 68.2 reduce-scatter.16
  721.0 38.3 all-gather.16
where the time goes:
time: 771 us; the launch traced here: 769 us
  waiting for transfers between devices  648 us (84%)
  matrix products  48.7 us (6%)
  other arithmetic  27.9 us (4%)
  between operations  21.1 us (3%)
  local copies, waits for them, and re-layouts  14.9 us (2%)
  starting transfers between devices  8.26 us (1%)
    reduce_scatter x3, waiting for transfers between devices, per_device(): lax.psum_scatter(own_part, 'tp', scatter_dimension=1, tiled=True)  205 us
    reduce_scatter x3, waiting for transfers between devices, per_device(): lax.psum_scatter(spare_part, 'tp', scatter_dimension=1, tiled=True)  196 us
    all_gather x3, waiting for transfers between devices, per_device(): entire_source_lines = lax.all_gather(x_sh, 'tp', axis=1, tiled=True)  116 us
    all_gather x3, waiting for transfers between devices, per_device(): ya_full = lax.all_gather(ya_sh, 'tp', axis=1, tiled=True)  108 us
    dot_general x6, matrix products, attend(): jnp.dot(normed, w_in.reshape(w_in.shape[0], 3 * col_count), preferred_ele...  30.3 us
    ppermute x9, waiting for transfers between devices, shifted(): return lax.ppermute(value, axis, pairs)  24.2 us
    dot_general x6, matrix products, attend(): return jnp.dot(context, w_out, preferred_element_type=jnp.float32)  15.6 us
  transfers between devices with their start and end apart: 21, of which 19 were waited for; matrix products, arithmetic and copies ran while one was open for 2% of the time, Pallas kernels for 0%

commit v1 on v0

--- a/solution.py
+++ b/solution.py
@@ -6,6 +6,16 @@
 HD = 128
 TICKS = 3
 NORM_EPS = 1e-05
+
+
+def gather_by_hops(array, mesh_axis, along):
+    size = lax.axis_size(mesh_axis)
+    moving, blocks = (array, [array])
+    for _ in range(size - 1):
+        moving = lax.ppermute(moving, mesh_axis, [(i, (i + 1) % size) for i in range(size)])
+        blocks.insert(0, moving)
+    line = jnp.concatenate(blocks, axis=along)
+    return jnp.roll(line, (lax.axis_index(mesh_axis) + 1) * array.shape[along], axis=along)
 
 
 def shifted(value, axis, steps):
@@ -102,7 +112,7 @@
         near_rows = shifted(send_sh, "section", 1)
         far_rows = shifted(spare_sh, "section", 2)
         x_sh = jnp.where(is_lost, jnp.zeros_like(far_rows), jnp.where(is_next, far_rows, near_rows))
-        entire_source_lines = lax.all_gather(x_sh, "tp", axis=1, tiled=True)
+        entire_source_lines = gather_by_hops(x_sh, "tp", 1)
         standby_sh = far_rows
     return (entire_source_lines[None], standby_sh[None])
 

time: 771 us -> 810 us (1.051)
  waiting for transfers between devices: 648 us -> 693 us
    ppermute x0 -> x21, waiting for transfers between devices: none -> 166 us  [gather_by_hops(): lax.ppermute(moving, mesh_axis, [(i, (i + 1) % size) for i in range(size)])]
    all_gather x3 -> x0, waiting for transfers between devices: 116 us -> none  [per_device(): entire_source_lines = lax.all_gather(x_sh, 'tp', axis=1, tiled=True)]
  transfers between devices with their start and end apart: 21 -> 39, of which waited for: 19 -> 37; matrix products, arithmetic and copies ran while one was open for 2% -> 1% of each run, Pallas kernels for 0% -> 0%
where the time goes in v1:
time: 810 us; the launch traced here: 809 us
  waiting for transfers between devices  693 us (86%)
  matrix products  48.7 us (6%)
  other arithmetic  23.2 us (3%)
  between operations  21 us (3%)
  local copies, waits for them, and re-layouts  12.9 us (2%)
  starting transfers between devices  10.2 us (1%)
    reduce_scatter x3, waiting for transfers between devices, per_device(): lax.psum_scatter(own_part, 'tp', scatter_dimension=1, tiled=True)  200 us
    reduce_scatter x3, waiting for transfers between devices, per_device(): lax.psum_scatter(spare_part, 'tp', scatter_dimension=1, tiled=True)  195 us
    ppermute x21, waiting for transfers between devices, gather_by_hops(): lax.ppermute(moving, mesh_axis, [(i, (i + 1) % size) for i in range(size)])  166 us
    all_gather x3, waiting for transfers between devices, per_device(): ya_full = lax.all_gather(ya_sh, 'tp', axis=1, tiled=True)  108 us
    dot_general x6, matrix products, attend(): jnp.dot(normed, w_in.reshape(w_in.shape[0], 3 * col_count), preferred_ele...  30.3 us
    ppermute x9, waiting for transfers between devices, shifted(): return lax.ppermute(value, axis, pairs)  24.1 us
  transfers between devices with their start and end apart: 39, of which 37 were waited for; matrix products, arithmetic and copies ran while one was open for 1% of the time, Pallas kernels for 0%

profile of v1, /device:TPU:0, one launch (start us, length us, event | category | flops | bytes accessed | tf_op | source)
XLA Modules:
  0.0 809.0 jit_solution(16168596121461015605)
XLA Ops:
  7.2 8.8 %copy.42 = bf16[1,4096,3,256]{1,3,2,0:T(8,128)(2,1)} copy(bf16[1,4096,3,256]{3,1,2,0:T(8,128)(2,1)} %param.17) | data formatting | bytes 12582912 | tf_op args[4]
  16.1 2.4 collective-permute-start.1
  19.9 5.2 convolution_convert_fusion.7
  26.5 1.8 fusion.107
  29.1 68.7 %reduce-scatter.7.cloned.1.call-done = f32[128,512]{1,0:T(8,128)} async-done(((f32[128,4096]{1,0:T(8,128)}), f32[128,512]{1,0:T(8,128)}) %reduce-scatter.7.cloned.1.call-update) | async-done | bytes 262160 | tf_op jit(solution)/shard_map/reduce_scatter | solution.py:95
  97.8 1.6 fusion.90
  100.3 9.4 %collective-permute-done = bf16[4096]{0:T(1024)(128)(2,1)S(1)} collective-permute-done((bf16[4096]{0:T(1024)(128)(2,1)S(1)}, bf16[4096]{0:T(1024)(128)(2,1)S(1)}, u32[]{:S(2)}, u32[]{:S(2)}) %collective-permute-start) | collective-permute-done | bytes 8224 | tf_op jit(solution)/shard_map/ppermute | solution.py:24
  109.7 29.2 %all-gather.4.cloned.1.call-done = bf16[128,4096]{1,0:T(8,128)(2,1)} async-done(((bf16[128,512]{1,0:T(8,128)(2,1)}), bf16[128,4096]{1,0:T(8,128)(2,1)}) %all-gather.4.cloned.1.call-update) | async-done | bytes 1048592 | tf_op jit(solution)/shard_map/all_gather | solution.py:97
  138.9 12.4 %conditional.2 = (f32[128,4096]{1,0:T(8,128)}) conditional(s32[]{:T(128)} %convert_element_type.183, () %tuple.21, (bf16[128,4096]{1,0:T(8,128)(2,1)}, bf16[4096]{0:T(1024)(128)(2,1)S(1)}, bf16[4096,3,256]{0,2,1:T(8,128)(2,1)}, bf16[256,4096]{1,0:T(8,128)(2,1)}) %tuple.22), branch_computations={%region_5.6_spmd, %region_6.11_spmd} | conditional | flops 1096667776 | bytes 19741220 | solution.py:101
  138.9 1.5 convert_reduce_fusion
  140.5 1.7 fusion.3
  142.2 5.0 convolution_convert_fusion
  148.0 3.4 fusion.124
  154.6 64.0 %reduce-scatter.9.cloned.1.call-done = f32[128,512]{1,0:T(8,128)} async-done(((f32[128,4096]{1,0:T(8,128)}), f32[128,512]{1,0:T(8,128)}) %reduce-scatter.9.cloned.1.call-update) | async-done | bytes 262160 | tf_op jit(solution)/shard_map/reduce_scatter | solution.py:105
  218.5 1.1 bitcast_select_fusion.2
  219.6 1.5 collective-permute-start.3
  221.2 4.0 collective-permute-done.3
  226.7 7.1 collective-permute-done.5
  233.8 7.7 collective-permute-done.6
  241.5 7.7 collective-permute-done.7
  249.1 7.9 collective-permute-done.8
  257.0 9.0 %collective-permute-done.9 = bf16[128,512]{1,0:T(8,128)(2,1)S(1)} collective-permute-done((bf16[128,512]{1,0:T(8,128)(2,1)S(1)}, bf16[128,512]{1,0:T(8,128)(2,1)S(1)}, u32[]{:S(2)}, u32[]{:S(2)}) %collective-permute-start.9) | collective-permute-done | bytes 131104 | tf_op jit(solution)/shard_map/ppermute | solution.py:15
  266.1 8.2 %collective-permute-done.10 = bf16[128,512]{1,0:T(8,128)(2,1)S(1)} collective-permute-done((bf16[128,512]{1,0:T(8,128)(2,1)S(1)}, bf16[128,512]{1,0:T(8,128)(2,1)S(1)}, u32[]{:S(2)}, u32[]{:S(2)}) %collective-permute-start.10) | collective-permute-done | bytes 131104 | tf_op jit(solution)/shard_map/ppermute | solution.py:15
  274.3 7.7 collective-permute-done.11
  283.2 5.0 convolution_convert_fusion.6
  289.0 1.8 fusion.105
  291.1 65.5 %reduce-scatter.11.cloned.1.call-done = f32[128,512]{1,0:T(8,128)} async-done(((f32[128,4096]{1,0:T(8,128)}), f32[128,512]{1,0:T(8,128)}) %reduce-scatter.11.cloned.1.call-update) | async-done | bytes 262160 | tf_op jit(solution)/shard_map/reduce_scatter | solution.py:95
  356.6 1.6 add_convert_fusion.3
  358.3 39.2 %all-gather.6.cloned.1.call-done = bf16[128,4096]{1,0:T(8,128)(2,1)} async-done(((bf16[128,512]{1,0:T(8,128)(2,1)}), bf16[128,4096]{1,0:T(8,128)(2,1)}) %all-gather.6.cloned.1.call-update) | async-done | bytes 1048592 | tf_op jit(solution)/shard_map/all_gather | solution.py:97
  397.5 12.4 %conditional.3 = (f32[128,4096]{1,0:T(8,128)}) conditional(s32[]{:T(128)} %convert_element_type.183, () %tuple.23, (bf16[128,4096]{1,0:T(8,128)(2,1)}, bf16[4096]{0:T(1024)(128)(2,1)S(1)}, bf16[4096,3,256]{0,2,1:T(8,128)(2,1)}, bf16[256,4096]{1,0:T(8,128)(2,1)}) %tuple.24), branch_computations={%region_17.19_spmd, %region_18.24_spmd} | conditional | flops 1096667776 | bytes 19741220 | solution.py:101
  397.5 1.5 convert_reduce_fusion.1
  399.1 1.7 fusion.19
  400.8 5.0 convolution_convert_fusion.2
  406.6 3.4 fusion.125
  412.0 65.2 %reduce-scatter.13.cloned.1.call-done = f32[128,512]{1,0:T(8,128)} async-done(((f32[128,4096]{1,0:T(8,128)}), f32[128,512]{1,0:T(8,128)}) %reduce-scatter.13.cloned.1.call-update) | async-done | bytes 262160 | tf_op jit(solution)/shard_map/reduce_scatter | solution.py:105
  478.2 1.5 collective-permute-start.12
  479.7 4.0 collective-permute-done.12
  485.2 7.2 collective-permute-done.14
  492.4 7.7 collective-permute-done.15
  500.1 7.7 collective-permute-done.16
  507.7 7.9 collective-permute-done.17
  515.6 9.0 %collective-permute-done.18 = bf16[128,512]{1,0:T(8,128)(2,1)S(1)} collective-permute-done((bf16[128,512]{1,0:T(8,128)(2,1)S(1)}, bf16[128,512]{1,0:T(8,128)(2,1)S(1)}, u32[]{:S(2)}, u32[]{:S(2)}) %collective-permute-start.18) | collective-permute-done | bytes 131104 | tf_op jit(solution)/shard_map/ppermute | solution.py:15
  524.7 8.2 %collective-permute-done.19 = bf16[128,512]{1,0:T(8,128)(2,1)S(1)} collective-permute-done((bf16[128,512]{1,0:T(8,128)(2,1)S(1)}, bf16[128,512]{1,0:T(8,128)(2,1)S(1)}, u32[]{:S(2)}, u32[]{:S(2)}) %collective-permute-start.19) | collective-permute-done | bytes 131104 | tf_op jit(solution)/shard_map/ppermute | solution.py:15
  532.9 7.7 collective-permute-done.20
  541.8 5.0 convolution_convert_fusion.5
  547.6 1.8 fusion.103
  549.5 65.7 %reduce-scatter.15.cloned.1.call-done = f32[128,512]{1,0:T(8,128)} async-done(((f32[128,4096]{1,0:T(8,128)}), f32[128,512]{1,0:T(8,128)}) %reduce-scatter.15.cloned.1.call-update) | async-done | bytes 262160 | tf_op jit(solution)/shard_map/reduce_scatter | solution.py:95
  615.2 1.6 add_convert_fusion.1
  616.9 39.4 %all-gather.8.cloned.1.call-done = bf16[128,4096]{1,0:T(8,128)(2,1)} async-done(((bf16[128,512]{1,0:T(8,128)(2,1)}), bf16[128,4096]{1,0:T(8,128)(2,1)}) %all-gather.8.cloned.1.call-update) | async-done | bytes 1048592 | tf_op jit(solution)/shard_map/all_gather | solution.py:97
  656.2 1.5 convert_reduce_fusion.3
  657.8 1.7 fusion.42
  659.5 5.0 convolution_convert_fusion.4
  665.2 3.4 fusion.126
  670.8 65.9 %reduce-scatter.17.cloned.1.call-done = f32[128,512]{1,0:T(8,128)} async-done(((f32[128,4096]{1,0:T(8,128)}), f32[128,512]{1,0:T(8,128)}) %reduce-scatter.17.cloned.1.call-update) | async-done | bytes 262160 | tf_op jit(solution)/shard_map/reduce_scatter | solution.py:105
  737.7 1.6 collective-permute-start.21
  739.3 3.9 collective-permute-done.21
  744.8 7.1 collective-permute-done.23
  751.9 7.7 collective-permute-done.24
  759.6 7.7 collective-permute-done.25
  767.2 7.9 collective-permute-done.26
  775.2 9.1 %collective-permute-done.27 = bf16[128,512]{1,0:T(8,128)(2,1)S(1)} collective-permute-done((bf16[128,512]{1,0:T(8,128)(2,1)S(1)}, bf16[128,512]{1,0:T(8,128)(2,1)S(1)}, u32[]{:S(2)}, u32[]{:S(2)}) %collective-permute-start.27) | collective-permute-done | bytes 131104 | tf_op jit(solution)/shard_map/ppermute | solution.py:15
  784.2 8.2 %collective-permute-done.28 = bf16[128,512]{1,0:T(8,128)(2,1)S(1)} collective-permute-done((bf16[128,512]{1,0:T(8,128)(2,1)S(1)}, bf16[128,512]{1,0:T(8,128)(2,1)S(1)}, u32[]{:S(2)}, u32[]{:S(2)}) %collective-permute-start.28) | collective-permute-done | bytes 131104 | tf_op jit(solution)/shard_map/ppermute | solution.py:15
  792.4 7.7 collective-permute-done.29
  800.2 1.5 fusion.70
  (170 shorter events, 19.0 us)
Async XLA Ops:
  7.2 11.9 %copy-start.11 = (bf16[1,4096]{1,0:T(2,128)(2,1)S(1)}, bf16[1,4096]{1,0:T(2,128)(2,1)}, u32[]{:S(2)}) copy-start(bf16[1,4096]{1,0:T(2,128)(2,1)} %param.19) | copy-start | bytes 24580
  7.2 12.0 %copy-start.1 = (bf16[1,128,4096]{2,1,0:T(8,128)(2,1)S(1)}, bf16[1,128,4096]{2,1,0:T(8,128)(2,1)}, u32[]{:S(2)}) copy-start(bf16[1,128,4096]{2,1,0:T(8,128)(2,1)} %param.13) | copy-start | bytes 3145732
  7.2 90.7 %reduce-scatter.7.cloned.1.call-start = ((), (), s32[]{:S(2)}) async-start(), calls=%async_computation.6 | async-start | bytes 2359296 | tf_op jit(solution)/shard_map/reduce_scatter | solution.py:95
  16.1 122.9 %collective-permute-start.1 = (bf16[4096,3,256]{0,2,1:T(8,128)(2,1)}, bf16[4096,3,256]{0,2,1:T(8,128)(2,1)}, u32[]{:S(2)}, u32[]{:S(2)}) collective-permute-start(bf16[4096,3,256]{0,2,1:T(8,128)(2,1)} %bitcast.142), channel_id=1, source_target_pairs={{0,24},{8,0},{16,8},{24,16},{1,25},{9,1},{17,9},{25,17},{2,26},{10... | collective-permute-start | bytes 18874376 | tf_op jit(solution)/shard_map/ppermute | solution.py:24
  19.2 0.7 copy-start.9
  19.8 6.7 copy-start
  28.3 110.6 %all-gather.4.cloned.1.call-start = ((), (), s32[]{:S(2)}) async-start(), calls=%async_computation.7 | async-start | bytes 1179648 | tf_op jit(solution)/shard_map/all_gather | solution.py:97
  28.4 81.3 %collective-permute-start.2 = (bf16[256,4096]{1,0:T(8,128)(2,1)S(1)}, bf16[256,4096]{1,0:T(8,128)(2,1)}, u32[]{:S(2)}, u32[]{:S(2)}) collective-permute-start(bf16[256,4096]{1,0:T(8,128)(2,1)S(1)} %bitcast.141), channel_id=1, source_target_pairs={{0,24},{8,0},{16,8},{24,16},{1,25},{9,1},{17,9},{25,17},{2,26},{10... | collective-permute-start | bytes 6291464 | tf_op jit(solution)/shard_map/ppermute | solution.py:24
  99.5 119.0 %reduce-scatter.9.cloned.1.call-start = ((), (), s32[]{:S(2)}) async-start(), calls=%async_computation.8 | async-start | bytes 2359296 | tf_op jit(solution)/shard_map/reduce_scatter | solution.py:105
  99.6 10.2 %collective-permute-start = (bf16[4096]{0:T(1024)(128)(2,1)S(1)}, bf16[4096]{0:T(1024)(128)(2,1)S(1)}, u32[]{:S(2)}, u32[]{:S(2)}) collective-permute-start(bf16[4096]{0:T(1024)(128)(2,1)S(1)} %reduce.1), channel_id=1, source_target_pairs={{0,24},{8,0},{16,8},{24,16},{1,25},{9,1},{17,9},{25,17},{2,26},{10... | collective-permute-start | bytes 24584 | tf_op jit(solution)/shard_map/ppermute | solution.py:24
  138.9 3.2 copy-start.2
  151.4 0.7 copy-start.13
  151.4 67.2 %copy-start.5 = (bf16[128,512]{1,0:T(8,128)(2,1)S(1)}, bf16[128,512]{1,0:T(8,128)(2,1)}, u32[]{:S(2)}) copy-start(bf16[128,512]{1,0:T(8,128)(2,1)} %fusion.90) | copy-start | bytes 393220
  151.4 205.2 %reduce-scatter.11.cloned.1.call-start = ((), (), s32[]{:S(2)}) async-start(), calls=%async_computation.9 | async-start | bytes 2359296 | tf_op jit(solution)/shard_map/reduce_scatter | solution.py:95
  219.6 5.5 collective-permute-start.3
  221.2 4.9 collective-permute-start.4
  226.1 7.7 collective-permute-start.5
  233.8 7.7 collective-permute-start.6
  241.5 7.7 collective-permute-start.7
  249.1 7.9 collective-permute-start.8
  257.0 9.0 %collective-permute-start.9 = (bf16[128,512]{1,0:T(8,128)(2,1)S(1)}, bf16[128,512]{1,0:T(8,128)(2,1)S(1)}, u32[]{:S(2)}, u32[]{:S(2)}) collective-permute-start(bf16[128,512]{1,0:T(8,128)(2,1)S(1)} %collective-permute-done.8), channel_id=1, source_target_pairs={{0,1},{1,2},{2,3},{3,4},{4,5},{5,6},{6,7},{7,0},{8,9},{9,10},{10,1... | collective-permute-start | bytes 393224 | tf_op jit(solution)/shard_map/ppermute | solution.py:15
  266.1 8.2 %collective-permute-start.10 = (bf16[128,512]{1,0:T(8,128)(2,1)S(1)}, bf16[128,512]{1,0:T(8,128)(2,1)S(1)}, u32[]{:S(2)}, u32[]{:S(2)}) collective-permute-start(bf16[128,512]{1,0:T(8,128)(2,1)S(1)} %collective-permute-done.9), channel_id=1, source_target_pairs={{0,1},{1,2},{2,3},{3,4},{4,5},{5,6},{6,7},{7,0},{8,9},{9,10},{10,1... | collective-permute-start | bytes 393224 | tf_op jit(solution)/shard_map/ppermute | solution.py:15
  274.3 7.7 collective-permute-start.11
  282.0 1.2 copy-start.10
  283.2 5.3 copy-start.12
  290.9 106.7 %all-gather.6.cloned.1.call-start = ((), (), s32[]{:S(2)}) async-start(), calls=%async_computation.10 | async-start | bytes 1179648 | tf_op jit(solution)/shard_map/all_gather | solution.py:97
  358.2 118.9 %reduce-scatter.13.cloned.1.call-start = ((), (), s32[]{:S(2)}) async-start(), calls=%async_computation.11 | async-start | bytes 2359296 | tf_op jit(solution)/shard_map/reduce_scatter | solution.py:105
  397.5 3.2 copy-start.3
  410.0 67.2 %copy-start.6 = (bf16[128,512]{1,0:T(8,128)(2,1)S(1)}, bf16[128,512]{1,0:T(8,128)(2,1)}, u32[]{:S(2)}) copy-start(bf16[128,512]{1,0:T(8,128)(2,1)} %add_convert_fusion.3) | copy-start | bytes 393220
  410.0 67.2 %copy-start.8 = (bf16[4,128,512]{2,1,0:T(8,128)(2,1)S(1)}, bf16[4,128,512]{2,1,0:T(8,128)(2,1)}, u32[]{:S(2)}) copy-start(bf16[4,128,512]{2,1,0:T(8,128)(2,1)} %param.14) | copy-start | bytes 1572868
  410.0 205.1 %reduce-scatter.15.cloned.1.call-start = ((), (), s32[]{:S(2)}) async-start(), calls=%async_computation.12 | async-start | bytes 2359296 | tf_op jit(solution)/shard_map/reduce_scatter | solution.py:95
  478.2 5.5 collective-permute-start.12
  479.7 4.9 collective-permute-start.13
  484.7 7.7 collective-permute-start.14
  492.4 7.7 collective-permute-start.15
  500.0 7.7 collective-permute-start.16
  507.7 7.9 collective-permute-start.17
  515.6 9.0 %collective-permute-start.18 = (bf16[128,512]{1,0:T(8,128)(2,1)S(1)}, bf16[128,512]{1,0:T(8,128)(2,1)S(1)}, u32[]{:S(2)}, u32[]{:S(2)}) collective-permute-start(bf16[128,512]{1,0:T(8,128)(2,1)S(1)} %collective-permute-done.17), channel_id=1, source_target_pairs={{0,1},{1,2},{2,3},{3,4},{4,5},{5,6},{6,7},{7,0},{8,9},{9,10},{10,1... | collective-permute-start | bytes 393224 | tf_op jit(solution)/shard_map/ppermute | solution.py:15
  524.7 8.2 %collective-permute-start.19 = (bf16[128,512]{1,0:T(8,128)(2,1)S(1)}, bf16[128,512]{1,0:T(8,128)(2,1)S(1)}, u32[]{:S(2)}, u32[]{:S(2)}) collective-permute-start(bf16[128,512]{1,0:T(8,128)(2,1)S(1)} %collective-permute-done.18), channel_id=1, source_target_pairs={{0,1},{1,2},{2,3},{3,4},{4,5},{5,6},{6,7},{7,0},{8,9},{9,10},{10,1... | collective-permute-start | bytes 393224 | tf_op jit(solution)/shard_map/ppermute | solution.py:15
  532.9 7.7 collective-permute-start.20
  549.4 106.8 %all-gather.8.cloned.1.call-start = ((), (), s32[]{:S(2)}) async-start(), calls=%async_computation.13 | async-start | bytes 1179648 | tf_op jit(solution)/shard_map/all_gather | solution.py:97
  616.8 119.9 %reduce-scatter.17.cloned.1.call-start = ((), (), s32[]{:S(2)}) async-start(), calls=%async_computation.14 | async-start | bytes 2359296 | tf_op jit(solution)/shard_map/reduce_scatter | solution.py:105
  656.2 3.2 copy-start.4
  668.7 68.1 %copy-start.7 = (bf16[128,512]{1,0:T(8,128)(2,1)S(1)}, bf16[128,512]{1,0:T(8,128)(2,1)}, u32[]{:S(2)}) copy-start(bf16[128,512]{1,0:T(8,128)(2,1)} %add_convert_fusion.1) | copy-start | bytes 393220
  737.7 5.5 collective-permute-start.21
  739.3 4.9 collective-permute-start.22
  744.2 7.7 collective-permute-start.23
  751.9 7.7 collective-permute-start.24
  759.6 7.7 collective-permute-start.25
  767.2 7.9 collective-permute-start.26
  775.2 9.1 %collective-permute-start.27 = (bf16[128,512]{1,0:T(8,128)(2,1)S(1)}, bf16[128,512]{1,0:T(8,128)(2,1)S(1)}, u32[]{:S(2)}, u32[]{:S(2)}) collective-permute-start(bf16[128,512]{1,0:T(8,128)(2,1)S(1)} %collective-permute-done.26), channel_id=1, source_target_pairs={{0,1},{1,2},{2,3},{3,4},{4,5},{5,6},{6,7},{7,0},{8,9},{9,10},{10,1... | collective-permute-start | bytes 393224 | tf_op jit(solution)/shard_map/ppermute | solution.py:15
  784.2 8.2 %collective-permute-start.28 = (bf16[128,512]{1,0:T(8,128)(2,1)S(1)}, bf16[128,512]{1,0:T(8,128)(2,1)S(1)}, u32[]{:S(2)}, u32[]{:S(2)}) collective-permute-start(bf16[128,512]{1,0:T(8,128)(2,1)S(1)} %collective-permute-done.27), channel_id=1, source_target_pairs={{0,1},{1,2},{2,3},{3,4},{4,5},{5,6},{6,7},{7,0},{8,9},{9,10},{10,1... | collective-permute-start | bytes 393224 | tf_op jit(solution)/shard_map/ppermute | solution.py:15
  792.4 7.7 collective-permute-start.29
Sparse Core Ops, SparseCore 0:
  28.5 69.3 reduce-scatter.6
  100.5 38.4 all-gather.3
  151.5 66.9 reduce-scatter.8
  291.0 65.5 reduce-scatter.10
  359.1 38.4 all-gather.5
  410.1 67.0 reduce-scatter.12
  549.5 65.5 reduce-scatter.14
  617.8 38.4 all-gather.7
  668.8 67.8 reduce-scatter.16
